TPU v7x, 16 devices: a whole 2x2x2 slice. The times are simulated.
16 devices in a mesh: sp: 16 (over z, y, x, core).
Axes of the slice: x: 2, y: 2, z: 2, core: 2. Of those that a mesh axis runs over, the one named last changes fastest.
Arguments:
- hidden: bfloat16 [16, 1024, 2048], P(None, 'sp')
- d_out: bfloat16 [16, 1024, 2048], P(None, 'sp')
- w_query: bfloat16 [2048, 16, 128], replicated
- w_key: bfloat16 [2048, 128], replicated
- w_value: bfloat16 [2048, 128], replicated
- w_out: bfloat16 [16, 128, 2048], replicated
Outputs:
- output 1: bfloat16 [16, 1024, 2048], P(None, 'sp')
- output 2: bfloat16 [16, 1024, 2048], P(None, 'sp')
- output 3: float32 [2048, 16, 128], replicated
- output 4: float32 [2048, 128], replicated
- output 5: float32 [2048, 128], replicated
- output 6: float32 [16, 128, 2048], replicated
All inputs are finite; a program needn't handle non-finite values.
Results may differ from a plain program's by a relative error of at most 0.0196.
Values are sent between devices in bfloat16 or wider.
A program may use at most 1 GiB of HBM per device.

v0:
```python
import jax
import jax.numpy as jnp
from jax import lax
from jax.sharding import PartitionSpec as P


def rope_tables(positions, head_dim):
    half_dim = head_dim // 2
    inv_freq = 10000.0 ** (-(jnp.arange(half_dim).astype(jnp.float32) * 2.0) / head_dim)
    angles = positions.astype(jnp.float32)[:, None] * inv_freq[None, :]
    return jnp.cos(angles), jnp.sin(angles)


def rotate(values, cos_tab, sin_tab):
    half_dim = values.shape[-1] // 2
    lead_half, tail_half = values[..., :half_dim], values[..., half_dim:]
    return jnp.concatenate([lead_half * cos_tab - tail_half * sin_tab, tail_half * cos_tab + lead_half * sin_tab], axis=-1)


def rotate_back(cotangent, cos_tab, sin_tab):
    half_dim = cotangent.shape[-1] // 2
    lead_half, tail_half = cotangent[..., :half_dim], cotangent[..., half_dim:]
    return jnp.concatenate([lead_half * cos_tab + tail_half * sin_tab, tail_half * cos_tab - lead_half * sin_tab], axis=-1)


def causal_softmax(scores):
    row_max = jnp.max(scores, axis=-1, keepdims=True)
    expo_vals = jnp.exp(scores - row_max)
    return expo_vals / jnp.sum(expo_vals, axis=-1, keepdims=True)


def solution(mesh):
    axis_size = mesh.shape['sp']
    seq_spec = P(None, 'sp', None)
    rep_spec = P()

    def local_step(hidden, d_out, w_query, w_key, w_value, w_out):
        local_len = hidden.shape[1]
        head_dim = w_key.shape[1]
        seq_len = local_len * axis_size
        score_scale = head_dim ** -0.5
        positions = lax.axis_index('sp') * local_len + jnp.arange(local_len)
        cos_tab, sin_tab = rope_tables(positions, head_dim)
        q_proj = jnp.einsum('bld,dhe->blhe', hidden, w_query, preferred_element_type=jnp.float32).astype(jnp.bfloat16)
        k_proj = jnp.einsum('bld,de->ble', hidden, w_key, preferred_element_type=jnp.float32).astype(jnp.bfloat16)
        v_proj = jnp.einsum('bld,de->ble', hidden, w_value, preferred_element_type=jnp.float32).astype(jnp.bfloat16)
        q_rot = rotate(q_proj.astype(jnp.float32), cos_tab[:, None, :], sin_tab[:, None, :]).astype(jnp.bfloat16)
        k_rot = rotate(k_proj.astype(jnp.float32), cos_tab, sin_tab).astype(jnp.bfloat16)
        q_heads = lax.all_to_all(q_rot, 'sp', 2, 1, tiled=True)
        kv_full = lax.all_gather(jnp.stack([k_rot, v_proj]), 'sp', axis=2, tiled=True)
        k_full, v_full = kv_full[0], kv_full[1]
        causal = jnp.arange(seq_len)[:, None] >= jnp.arange(seq_len)[None, :]
        scores = jnp.einsum('bqhe,bke->bhqk', q_heads, k_full, preferred_element_type=jnp.float32) * score_scale
        attn_prob = causal_softmax(jnp.where(causal, scores, -jnp.inf))
        prob_half = attn_prob.astype(jnp.bfloat16)
        attn_heads = jnp.einsum('bhqk,bke->bqhe', prob_half, v_full, preferred_element_type=jnp.float32).astype(jnp.bfloat16)
        attn = lax.all_to_all(attn_heads, 'sp', 1, 2, tiled=True)
        attn_out = jnp.einsum('blhe,hed->bld', attn, w_out, preferred_element_type=jnp.float32).astype(jnp.bfloat16)
        d_attn = jnp.einsum('bld,hed->blhe', d_out, w_out, preferred_element_type=jnp.float32).astype(jnp.bfloat16)
        grad_w_out = jnp.einsum('blhe,bld->hed', attn, d_out, preferred_element_type=jnp.float32)
        d_attn_heads = lax.all_to_all(d_attn, 'sp', 2, 1, tiled=True)
        row_delta = jnp.einsum('bqhe,bqhe->bhq', d_attn_heads, attn_heads, preferred_element_type=jnp.float32)
        d_prob = jnp.einsum('bqhe,bke->bhqk', d_attn_heads, v_full, preferred_element_type=jnp.float32)
        d_scores = (attn_prob * (d_prob - row_delta[..., None]) * score_scale).astype(jnp.bfloat16)
        dv_part = jnp.einsum('bhqk,bqhe->bke', prob_half, d_attn_heads, preferred_element_type=jnp.float32)
        dk_part = jnp.einsum('bhqk,bqhe->bke', d_scores, q_heads, preferred_element_type=jnp.float32)
        dq_heads = jnp.einsum('bhqk,bke->bqhe', d_scores, k_full, preferred_element_type=jnp.float32).astype(jnp.bfloat16)
        kv_grad = lax.psum_scatter(jnp.stack([dk_part, dv_part]), 'sp', scatter_dimension=2, tiled=True).astype(jnp.bfloat16)
        dq_rot = lax.all_to_all(dq_heads, 'sp', 1, 2, tiled=True)
        d_query = rotate_back(dq_rot.astype(jnp.float32), cos_tab[:, None, :], sin_tab[:, None, :]).astype(jnp.bfloat16)
        d_key = rotate_back(kv_grad[0].astype(jnp.float32), cos_tab, sin_tab).astype(jnp.bfloat16)
        d_value = kv_grad[1]
        d_hidden = (jnp.einsum('blhe,dhe->bld', d_query, w_query, preferred_element_type=jnp.float32) + jnp.einsum('ble,de->bld', d_key, w_key, preferred_element_type=jnp.float32) + jnp.einsum('ble,de->bld', d_value, w_value, preferred_element_type=jnp.float32)).astype(jnp.bfloat16)
        grad_w_query = jnp.einsum('bld,blhe->dhe', hidden, d_query, preferred_element_type=jnp.float32)
        grad_w_key = jnp.einsum('bld,ble->de', hidden, d_key, preferred_element_type=jnp.float32)
        grad_w_value = jnp.einsum('bld,ble->de', hidden, d_value, preferred_element_type=jnp.float32)
        grad_sums = lax.psum((grad_w_query, grad_w_key, grad_w_value, grad_w_out), 'sp')
        return (attn_out, d_hidden, grad_sums[0], grad_sums[1], grad_sums[2], grad_sums[3])

    return jax.shard_map(local_step, mesh=mesh, in_specs=(seq_spec, seq_spec, rep_spec, rep_spec, rep_spec, rep_spec), out_specs=(seq_spec, seq_spec, rep_spec, rep_spec, rep_spec, rep_spec), check_vma=False)
```

profile of v0, /device:TPU:0, one launch (start us, length us, event | category | flops | bytes accessed | tf_op | source)
XLA Modules:
  0.0 1008.4 jit_solution(2583437798039163144)
XLA Ops:
  16.7 12.6 %convert_convert_fusion = f32[16,64,16,128]{3,1,2,0:T(8,128)S(1)} fusion(bf16[2048,16,128]{2,1,0:T(8,128)(2,1)} %param.8, bf16[16,64,2048]{2,1,0:T(8,128)(2,1)} %param.6), kind=kOutput, calls=%fused_computation.46 | convolution fusion | flops 8594128896 | bytes 20971520 | tf_op jit(solution)/shard_map/bld,dhe->blhe/dot_general | solution.py:44
  37.8 5.6 all-to-all-start
  43.3 12.4 %fusion.38 = bf16[16,64,16,128]{3,1,2,0:T(8,128)(2,1)S(1)} fusion(bf16[16,128,2048]{2,1,0:T(8,128)(2,1)} %param.11, bf16[16,64,2048]{2,1,0:T(8,128)(2,1)} %param.7), kind=kOutput, calls=%fused_computation.52 | convolution fusion | flops 8592031744 | bytes 16777216 | tf_op jit(solution)/shard_map/bld,hed->blhe/dot_general | solution.py:59
  58.7 49.8 %all-to-all-done = bf16[16,64,16,128]{3,1,0,2:T(8,128)(2,1)} async-done(((bf16[16,64,16,128]{3,1,0,2:T(8,128)(2,1)}), bf16[16,64,16,128]{3,1,0,2:T(8,128)(2,1)}, u32[]{:S(2)}, u32[]{:S(2)}) %all-to-all-start) | async-done | bytes 4194336 | tf_op jit(solution)/shard_map/all_to_all | solution.py:49
  112.8 5.6 copy.40
  118.4 47.5 %all-to-all-done.2 = bf16[16,64,16,128]{3,1,0,2:T(8,128)(2,1)} async-done(((bf16[16,64,16,128]{3,1,0,2:T(8,128)(2,1)}), bf16[16,64,16,128]{3,1,0,2:T(8,128)(2,1)}, u32[]{:S(2)}, u32[]{:S(2)}) %all-to-all-start.2) | async-done | bytes 4194336 | tf_op jit(solution)/shard_map/all_to_all | solution.py:61
  166.0 5.6 copy.46
  171.5 6.8 copy.63
  178.4 26.6 %fusion.4 = (f32[16,1024]{1,0:T(8,128)S(1)}, f32[16,1024,1024]{2,1,0:T(8,128)}) fusion(pred[1024,1024]{0,1:T(8,128)(4,1)S(1)} %iota_compare_fusion, bf16[16,1024,128]{2,1,0:T(8,128)(2,1)} %bitcast.201, bf16[2,16,1024,128]{3,2,1,0:T(8,128)(2,1)} %all-gather.2.cloned.1.call-done), kind=kOutput, calls=%fused_computation.8 | convolution fusion | flops 4345282560 | bytes 76611584 | tf_op jit(solution)/shard_map/bqhe,bke->bhqk/dot_general | solution.py:53
  205.0 21.6 %fusion.3 = f32[16,1024]{1,0:T(8,128)S(1)} fusion(f32[16,1024,1024]{2,1,0:T(8,128)} %get-tuple-element.39, f32[16,1024]{1,0:T(8,128)S(1)} %get-tuple-element.38, pred[1024,1024]{0,1:T(8,128)(4,1)S(1)} %iota_compare_fusion), kind=kLoop, calls=%fused_computation.7 | loop fusion | flops 67092480 | bytes 68288512 | tf_op jit(solution)/shard_map/reduce_sum | solution.py:29
  226.6 30.1 %fusion.31 = f32[1,16,1024,128]{3,2,1,0:T(8,128)} fusion(bf16[16,1024,128]{2,1,0:T(8,128)(2,1)} %bitcast.204, f32[16,1024]{1,0:T(8,128)S(1)} %fusion.3, f32[16,1024]{1,0:T(8,128)S(1)} %get-tuple-element.38, f32[16,1024,1024]{2,1,0:T(8,128)} %get-tuple-element.39, pred[1024,1024]{0,1:T(8,128)(4,1)S(1)} %iota_compare_fusion), kind=kOutput, calls=%fused_computation.50 | convolution fusion | flops 4378853376 | bytes 80871424 | tf_op jit(solution)/shard_map/bhqk,bqhe->bke/dot_general | solution.py:65
  256.7 31.6 %multiply_reduce_fusion = (f32[16,1024]{1,0:T(8,128)S(1)}, bf16[16,128,1024]{2,1,0:T(8,128)(2,1)}) fusion(f32[16,1024,128]{1,2,0:T(8,128)} %copy.63, f32[16,1024]{1,0:T(8,128)S(1)} %fusion.3, f32[16,1024]{1,0:T(8,128)S(1)} %get-tuple-element.38, f32[16,1024,1024]{2,1,0:T(8,128)} %get-tuple-element.39, pred[1024,1024]{0,1:T(8,128)(4,1)S(1)} %iota_compare_fusion, ...), kind=kOutput, calls=%fused_computation.28 | convolution fusion | flops 4387225600 | bytes 85131264 | tf_op jit(solution)/shard_map/bhqk,bke->bqhe/dot_general | solution.py:56
  288.2 42.0 %fusion.5 = bf16[16,1024,1024]{1,2,0:T(8,128)(2,1)} fusion(f32[16,1024]{1,0:T(8,128)S(1)} %get-tuple-element.40, f32[16,1024]{1,0:T(8,128)S(1)} %fusion.3, f32[16,1024]{1,0:T(8,128)S(1)} %get-tuple-element.38, f32[16,1024,1024]{2,1,0:T(8,128)} %get-tuple-element.39, pred[1024,1024]{0,1:T(8,128)(4,1)S(1)} %iota_compare_fusion, ...), kind=kOutput, calls=%fused_computation.9 | convolution fusion | flops 4429185024 | bytes 110297088 | tf_op jit(solution)/shard_map/bqhe,bke->bhqk/dot_general | solution.py:63
  330.3 18.4 %convolution_bitcast_fusion.2 = f32[1,16,1024,128]{3,2,1,0:T(8,128)} fusion(bf16[16,1024,1024]{1,2,0:T(8,128)(2,1)} %fusion.5, bf16[16,1024,128]{2,1,0:T(8,128)(2,1)} %bitcast.202), kind=kOutput, calls=%fused_computation.51 | convolution fusion | flops 4294967296 | bytes 46137344 | tf_op jit(solution)/shard_map/bhqk,bqhe->bke/dot_general | solution.py:66
  348.7 11.5 %pad_maximum_fusion = f32[2,16,1024,128]{3,2,1,0:T(8,128)} fusion(f32[1,16,1024,128]{3,2,1,0:T(8,128)} %fusion.31, f32[1,16,1024,128]{3,2,1,0:T(8,128)} %convolution_bitcast_fusion.2), kind=kLoop, calls=%fused_computation.15 | loop fusion | flops 4194304 | bytes 33554432 | tf_op jit(solution)/shard_map/stack | solution.py:68
  360.2 16.5 %convert_bitcast_fusion = bf16[16,1024,1,128]{1,3,0,2:T(8,128)(2,1)} fusion(bf16[16,1024,1024]{1,2,0:T(8,128)(2,1)} %fusion.5, bf16[2,16,1024,128]{3,2,1,0:T(8,128)(2,1)} %all-gather.2.cloned.1.call-done), kind=kOutput, calls=%fused_computation.45 | convolution fusion | flops 4297064448 | bytes 41943040 | tf_op jit(solution)/shard_map/bhqk,bke->bqhe/dot_general | solution.py:67
  376.7 6.8 copy.49
  383.5 4.4 all-to-all-start.3
  388.0 6.8 copy.43
  394.8 87.7 %all-to-all-done.3 = bf16[16,1024,1,128]{3,0,2,1:T(8,128)(2,1)} async-done(((bf16[16,1024,1,128]{3,0,2,1:T(8,128)(2,1)}), bf16[16,1024,1,128]{3,0,2,1:T(8,128)(2,1)}, u32[]{:S(2)}, u32[]{:S(2)}) %all-to-all-start.3) | async-done | bytes 4194336 | tf_op jit(solution)/shard_map/all_to_all | solution.py:69
  486.1 6.5 copy.50
  492.6 87.9 %all-to-all-done.1 = bf16[16,1024,1,128]{3,0,2,1:T(8,128)(2,1)} async-done(((bf16[16,1024,1,128]{3,0,2,1:T(8,128)(2,1)}), bf16[16,1024,1,128]{3,0,2,1:T(8,128)(2,1)}, u32[]{:S(2)}, u32[]{:S(2)}) %all-to-all-start.1) | async-done | bytes 4194336 | tf_op jit(solution)/shard_map/all_to_all | solution.py:57
  585.7 4.4 add_convert_fusion
  590.1 16.4 %convolution_bitcast_fusion.1 = f32[2048,16,128]{0,2,1:T(8,128)} fusion(bf16[16,64,2048]{2,1,0:T(8,128)(2,1)S(1)} %copy-done.2, bf16[16,64,16,64]{3,1,2,0:T(8,128)(2,1)} %get-tuple-element.29, bf16[16,64,16,64]{3,1,2,0:T(8,128)(2,1)S(1)} %get-tuple-element.28), kind=kOutput, calls=%fused_computation.36 | convolution fusion | flops 8598323200 | bytes 25165824 | tf_op jit(solution)/shard_map/bld,blhe->dhe/dot_general | solution.py:74
  606.6 11.6 %convolution_bitcast_fusion = f32[16,128,2048]{2,1,0:T(8,128)} fusion(bf16[16,64,16,128]{3,1,2,0:T(8,128)(2,1)S(1)} %bitcast.206, bf16[16,64,2048]{2,1,0:T(8,128)(2,1)S(1)} %copy-done.19), kind=kOutput, calls=%fused_computation.35 | convolution fusion | flops 8589934592 | bytes 25165824 | tf_op jit(solution)/shard_map/blhe,bld->hed/dot_general | solution.py:60
  618.2 11.7 %reduce-scatter.2.cloned.1.call-done = f32[2,16,64,128]{3,2,1,0:T(8,128)} async-done(((f32[2,16,1024,128]{3,2,1,0:T(8,128)}), f32[2,16,64,128]{3,2,1,0:T(8,128)}) %reduce-scatter.2.cloned.1.call-update) | async-done | bytes 1048592 | tf_op jit(solution)/shard_map/reduce_scatter | solution.py:68
  631.5 4.1 convolution_bitcast_fusion.3
  638.5 13.3 %bitcast_convert_fusion = bf16[16,64,2048]{2,1,0:T(8,128)(2,1)} fusion(bf16[16,64,16,128]{3,1,2,0:T(8,128)(2,1)} %bitcast.207, bf16[16,128,2048]{2,1,0:T(8,128)(2,1)} %param.11), kind=kOutput, calls=%fused_computation.19 | convolution fusion | flops 8592031744 | bytes 16777216 | tf_op jit(solution)/shard_map/blhe,hed->bld/dot_general | solution.py:58
  651.9 12.1 %fusion.17 = f32[16,64,2048,1]{2,1,3,0:T(8,128)S(1)} fusion(bf16[2048,16,128]{2,1,0:T(8,128)(2,1)} %param.8, bf16[16,64,16,64]{3,1,2,0:T(8,128)(2,1)S(1)} %copy-done.7, bf16[16,64,16,64]{3,1,2,0:T(8,128)(2,1)S(1)} %copy-done.6), kind=kOutput, calls=%fused_computation.24 | convolution fusion | flops 8598323200 | bytes 20971520 | tf_op jit(solution)/shard_map/blhe,dhe->bld/dot_general | solution.py:73
  669.7 299.5 %all-reduce.3.cloned.1.call-done = (f32[2048,16,128]{0,2,1:T(8,128)}, f32[2048,128]{0,1:T(8,128)}, f32[2048,128]{0,1:T(8,128)}, f32[16,128,2048]{2,1,0:T(8,128)}) async-done(((f32[2048,16,128]{0,2,1:T(8,128)}, f32[2048,128]{0,1:T(8,128)}, f32[2048,128]{0,1:T(8,128)}, f32[16,128,2048]{2,1,0:T(8,128)}), (f32[2048,16,128]{0,2,1:T(8,128)}, f32[2048,128]{0,1:T(8,128)}, f32[2048,128]{0,1:T(8,128)}, ...) | async-done | bytes 35651600 | tf_op jit(solution)/shard_map/psum | solution.py:77
  969.2 17.8 %copy.52 = f32[2048,16,128]{2,1,0:T(8,128)} copy(f32[2048,16,128]{0,2,1:T(8,128)} %get-tuple-element.24) | data formatting | bytes 33554432
  989.6 11.8 %copy.81 = f32[16,128,2048]{2,1,0:T(8,128)} copy(f32[16,128,2048]{2,1,0:T(8,128)} %get-tuple-element.47) | data formatting | bytes 33554432
  (70 shorter events, 46.6 us)
Async XLA Ops:
  7.2 1.0 copy-start
  7.2 171.2 %all-gather.2.cloned.1.call-start = ((), (), s32[]{:S(2)}) async-start(), calls=%async_computation.5 | async-start | bytes 8912896 | tf_op jit(solution)/shard_map/all_gather | solution.py:50
  15.4 13.9 %copy-start.14 = (f32[64,64]{1,0:T(8,128)}, f32[64,64]{1,0:T(8,128)S(1)}, u32[]{:S(2)}) copy-start(f32[64,64]{1,0:T(8,128)S(1)} %get-tuple-element.36) | copy-start | bytes 49156
  15.4 13.9 %copy-start.16 = (f32[64,64]{1,0:T(8,128)}, f32[64,64]{1,0:T(8,128)S(1)}, u32[]{:S(2)}) copy-start(f32[64,64]{1,0:T(8,128)S(1)} %get-tuple-element.37) | copy-start | bytes 49156
  37.8 70.7 %all-to-all-start = ((bf16[16,64,16,128]{3,1,0,2:T(8,128)(2,1)}), bf16[16,64,16,128]{3,1,0,2:T(8,128)(2,1)}, u32[]{:S(2)}, u32[]{:S(2)}) async-start(bf16[16,64,16,128]{3,1,0,2:T(8,128)(2,1)} %copy.39), calls=%async_computation | async-start | bytes 8388608 | tf_op jit(solution)/shard_map/all_to_all | solution.py:49
  108.5 57.5 %all-to-all-start.2 = ((bf16[16,64,16,128]{3,1,0,2:T(8,128)(2,1)}), bf16[16,64,16,128]{3,1,0,2:T(8,128)(2,1)}, u32[]{:S(2)}, u32[]{:S(2)}) async-start(bf16[16,64,16,128]{3,1,0,2:T(8,128)(2,1)} %copy.45), calls=%async_computation.2 | async-start | bytes 8388608 | tf_op jit(solution)/shard_map/all_to_all | solution.py:61
  112.5 517.5 %reduce-scatter.2.cloned.1.call-start = ((), (), s32[]{:S(2)}) async-start(), calls=%async_computation.6 | async-start | bytes 17825792 | tf_op jit(solution)/shard_map/reduce_scatter | solution.py:68
  383.5 98.9 %all-to-all-start.3 = ((bf16[16,1024,1,128]{3,0,2,1:T(8,128)(2,1)}), bf16[16,1024,1,128]{3,0,2,1:T(8,128)(2,1)}, u32[]{:S(2)}, u32[]{:S(2)}) async-start(bf16[16,1024,1,128]{3,0,2,1:T(8,128)(2,1)} %copy.49), calls=%async_computation.3 | async-start | bytes 8388608 | tf_op jit(solution)/shard_map/all_to_all | solution.py:69
  482.5 98.0 %all-to-all-start.1 = ((bf16[16,1024,1,128]{3,0,2,1:T(8,128)(2,1)}), bf16[16,1024,1,128]{3,0,2,1:T(8,128)(2,1)}, u32[]{:S(2)}, u32[]{:S(2)}) async-start(bf16[16,1024,1,128]{3,0,2,1:T(8,128)(2,1)} %copy.43), calls=%async_computation.1 | async-start | bytes 8388608 | tf_op jit(solution)/shard_map/all_to_all | solution.py:57
  486.0 97.9 %copy-start.15 = (f32[64,64]{1,0:T(8,128)S(1)}, f32[64,64]{1,0:T(8,128)}, u32[]{:S(2)}) copy-start(f32[64,64]{1,0:T(8,128)} %copy-done.14) | copy-start | bytes 49156
  486.0 97.9 %copy-start.17 = (f32[64,64]{1,0:T(8,128)S(1)}, f32[64,64]{1,0:T(8,128)}, u32[]{:S(2)}) copy-start(f32[64,64]{1,0:T(8,128)} %copy-done.16) | copy-start | bytes 49156
  486.0 483.1 %all-reduce.3.cloned.1.call-start = ((), (), s32[]{:S(2)}) async-start(), calls=%async_computation.7 | async-start | bytes 71303168 | tf_op jit(solution)/shard_map/psum | solution.py:77
  580.5 5.2 copy-start.1
  583.9 22.6 %copy-start.4 = (bf16[16,1024,1,128]{3,1,0,2:T(8,128)(2,1)}, bf16[16,1024,1,128]{3,1,0,2:T(8,128)(2,1)S(1)}, u32[]{:S(2)}) copy-start(bf16[16,1024,1,128]{3,1,0,2:T(8,128)(2,1)S(1)} %copy.44) | copy-start | bytes 12582916
  585.7 4.4 copy-start.2
  590.1 16.4 %copy-start.5 = (bf16[16,64,16,64]{3,1,2,0:T(8,128)(2,1)}, bf16[16,64,16,64]{3,1,2,0:T(8,128)(2,1)S(1)}, u32[]{:S(2)}) copy-start(bf16[16,64,16,64]{3,1,2,0:T(8,128)(2,1)S(1)} %get-tuple-element.28) | copy-start | bytes 6291460
  590.1 16.4 %copy-start.19 = (bf16[16,64,2048]{2,1,0:T(8,128)(2,1)S(1)}, bf16[16,64,2048]{2,1,0:T(8,128)(2,1)}, u32[]{:S(2)}) copy-start(bf16[16,64,2048]{2,1,0:T(8,128)(2,1)} %param.7) | copy-start | bytes 12582916
  630.0 6.7 copy-start.3
  631.4 4.5 copy-start.8
  635.9 0.7 copy-start.10
  635.9 0.8 copy-start.11
  638.5 13.3 %copy-start.6 = (bf16[16,64,16,64]{3,1,2,0:T(8,128)(2,1)S(1)}, bf16[16,64,16,64]{3,1,2,0:T(8,128)(2,1)}, u32[]{:S(2)}) copy-start(bf16[16,64,16,64]{3,1,2,0:T(8,128)(2,1)} %copy-done.5) | copy-start | bytes 6291460
  638.5 13.3 %copy-start.7 = (bf16[16,64,16,64]{3,1,2,0:T(8,128)(2,1)S(1)}, bf16[16,64,16,64]{3,1,2,0:T(8,128)(2,1)}, u32[]{:S(2)}) copy-start(bf16[16,64,16,64]{3,1,2,0:T(8,128)(2,1)} %get-tuple-element.29) | copy-start | bytes 6291460
  663.9 2.4 copy-start.9
  663.9 2.4 copy-start.18
  969.2 17.8 %copy-start.13 = (f32[2048,128]{0,1:T(8,128)S(1)}, f32[2048,128]{0,1:T(8,128)}, u32[]{:S(2)}) copy-start(f32[2048,128]{0,1:T(8,128)} %get-tuple-element.25) | copy-start | bytes 3145732
  969.2 19.1 %copy-start.12 = (f32[2048,128]{0,1:T(8,128)S(1)}, f32[2048,128]{0,1:T(8,128)}, u32[]{:S(2)}) copy-start(f32[2048,128]{0,1:T(8,128)} %get-tuple-element.26) | copy-start | bytes 3145732
Sparse Core Ops, SparseCore 0:
  16.8 92.2 all-gather.1
  360.3 269.6 reduce-scatter.1
  638.6 330.4 all-reduce.2
where the time goes:
time: 1020 us; the launch traced here: 1010 us
  waiting for transfers between devices  584 us (57%)
  matrix products  262 us (26%)
  local copies, waits for them, and re-layouts  83.2 us (8%)
  other arithmetic  46.4 us (5%)
  starting transfers between devices  17.6 us (2%)
  between operations  14.5 us (1%)
    psum x1, waiting for transfers between devices, local_step(): lax.psum((grad_w_query, grad_w_key, grad_w_value, grad_w_out), 'sp')  300 us
    all_to_all x1, waiting for transfers between devices, local_step(): attn = lax.all_to_all(attn_heads, 'sp', 1, 2, tiled=True)  87.9 us
    all_to_all x1, waiting for transfers between devices, local_step(): dq_rot = lax.all_to_all(dq_heads, 'sp', 1, 2, tiled=True)  87.7 us
    all_to_all x1, waiting for transfers between devices, local_step(): q_heads = lax.all_to_all(q_rot, 'sp', 2, 1, tiled=True)  49.8 us
    all_to_all x1, waiting for transfers between devices, local_step(): d_attn_heads = lax.all_to_all(d_attn, 'sp', 2, 1, tiled=True)  47.5 us
    unnamed x45, local copies, waits for them, and re-layouts  42.5 us
    dot_general x1, matrix products, local_step(): jnp.einsum('bqhe,bke->bhqk', d_attn_heads, v_full, preferred_element_type...  42 us
    dot_general x1, matrix products, local_step(): jnp.einsum('bhqk,bke->bqhe', prob_half, v_full, preferred_element_type=jn...  31.6 us
  transfers between devices with their start and end apart: 7, of which 6 were waited for; matrix products, arithmetic and copies ran while one was open for 16% of the time, Pallas kernels for 0%

commit v1 on v0

v1 whole, which is shorter than its diff:
```python
import functools

import jax
import jax.numpy as jnp
from jax import lax
from jax.experimental import pallas as pl
from jax.experimental.pallas import tpu as pltpu
from jax.sharding import PartitionSpec as P

F32 = jnp.float32
BF16 = jnp.bfloat16
LOG2E = 1.4426950408889634
NT = (((1,), (1,)), ((), ()))
TN = (((0,), (0,)), ((), ()))


def rope_tables(positions, head_dim):
    half_dim = head_dim // 2
    inv_freq = 10000.0 ** (-(jnp.arange(half_dim).astype(F32) * 2.0) / head_dim)
    angles = positions.astype(F32)[:, None] * inv_freq[None, :]
    return jnp.cos(angles), jnp.sin(angles)


def rotate(values, cos_tab, sin_tab):
    half_dim = values.shape[-1] // 2
    lead_half, tail_half = values[..., :half_dim], values[..., half_dim:]
    return jnp.concatenate([lead_half * cos_tab - tail_half * sin_tab, tail_half * cos_tab + lead_half * sin_tab], axis=-1)


def rotate_back(cotangent, cos_tab, sin_tab):
    half_dim = cotangent.shape[-1] // 2
    lead_half, tail_half = cotangent[..., :half_dim], cotangent[..., half_dim:]
    return jnp.concatenate([lead_half * cos_tab + tail_half * sin_tab, tail_half * cos_tab - lead_half * sin_tab], axis=-1)


def attn_kernel(n_tiles, scale, q_ref, do_ref, kv_ref, cos_ref, sin_ref, cap_ref, o_ref, dq_ref, dkv_ref, dk_acc, dv_acc):
    heads, length, dim = q_ref.shape
    ndev = kv_ref.shape[0]
    keys = ndev * length
    k = kv_ref[:, 0, 0].reshape(keys, dim)
    v = kv_ref[:, 1, 0].reshape(keys, dim)
    hpt = heads // n_tiles
    rows = hpt * length
    cosd = cos_ref[...][None]
    sind = sin_ref[...][None]
    for t in range(n_tiles):
        hs = pl.ds(t * hpt, hpt)
        qf = q_ref[hs].astype(F32)
        qr = (qf * cosd + pltpu.roll(qf, dim // 2, 2) * sind).astype(BF16).reshape(rows, dim)
        s = lax.dot_general(qr, k, NT, preferred_element_type=F32)
        s = jnp.minimum(s.reshape(hpt, length, keys), cap_ref[...][None]).reshape(rows, keys)
        m = jnp.max(s, axis=1, keepdims=True)
        e = jnp.exp2((s - m) * (scale * LOG2E))
        p = e * (1.0 / jnp.sum(e, axis=1, keepdims=True))
        pb = p.astype(BF16)
        ob = lax.dot(pb, v, preferred_element_type=F32).astype(BF16)
        o_ref[hs] = ob.reshape(hpt, length, dim)
        do = do_ref[hs].reshape(rows, dim)
        delta = jnp.sum(do.astype(F32) * ob.astype(F32), axis=1, keepdims=True)
        dp = lax.dot_general(do, v, NT, preferred_element_type=F32)
        ds = (p * (dp - delta) * scale).astype(BF16)
        dqr = lax.dot(ds, k, preferred_element_type=F32).astype(BF16).astype(F32).reshape(hpt, length, dim)
        dq_ref[hs] = (dqr * cosd - pltpu.roll(dqr, dim // 2, 2) * sind).astype(BF16)
        dv = lax.dot_general(pb, do, TN, preferred_element_type=F32)
        dk = lax.dot_general(ds, qr, TN, preferred_element_type=F32)
        if t == 0:
            dk_acc[...] = dk
            dv_acc[...] = dv
        elif t < n_tiles - 1:
            dk_acc[...] += dk
            dv_acc[...] += dv
        else:
            dkv_ref[:, 0, 0] = (dk_acc[...] + dk).reshape(ndev, length, dim)
            dkv_ref[:, 1, 0] = (dv_acc[...] + dv).reshape(ndev, length, dim)


def attention(q, do, kv_all, cos_tab, sin_tab, cap, scale):
    heads, tokens, dim = q.shape
    ndev, _, batch, length, _ = kv_all.shape
    keys = ndev * length
    rows_spec = pl.BlockSpec((heads, length, dim), lambda b: (0, b, 0))
    kv_spec = pl.BlockSpec((ndev, 2, 1, length, dim), lambda b: (0, 0, b, 0, 0))
    flops = 12 * batch * heads * length * keys * dim
    return pl.pallas_call(
        functools.partial(attn_kernel, 4, scale),
        grid=(batch,),
        in_specs=[rows_spec, rows_spec, kv_spec,
                  pl.BlockSpec((length, dim), lambda b: (0, 0)),
                  pl.BlockSpec((length, dim), lambda b: (0, 0)),
                  pl.BlockSpec((length, keys), lambda b: (0, 0))],
        out_specs=[rows_spec, rows_spec, kv_spec],
        out_shape=[jax.ShapeDtypeStruct(q.shape, BF16), jax.ShapeDtypeStruct(q.shape, BF16),
                   jax.ShapeDtypeStruct(kv_all.shape, F32)],
        scratch_shapes=[pltpu.VMEM((keys, dim), F32), pltpu.VMEM((keys, dim), F32)],
        compiler_params=pltpu.CompilerParams(vmem_limit_bytes=48 * 1024 * 1024),
        cost_estimate=pl.CostEstimate(flops=flops, bytes_accessed=40 * 1024 * 1024, transcendentals=batch * heads * length * keys),
        name="attn",
    )(q, do, kv_all, cos_tab, sin_tab, cap)


def solution(mesh):
    axis_size = mesh.shape['sp']
    seq_spec = P(None, 'sp', None)
    rep_spec = P()

    def local_step(hidden, d_out, w_query, w_key, w_value, w_out):
        batch, local_len, width = hidden.shape
        head_dim = w_key.shape[1]
        seq_len = local_len * axis_size
        tokens = batch * local_len
        score_scale = head_dim ** -0.5
        positions = lax.axis_index('sp') * local_len + jnp.arange(local_len)
        cos_tab, sin_tab = rope_tables(positions, head_dim)
        cos_full = jnp.concatenate([cos_tab, cos_tab], axis=-1)
        sin_full = jnp.concatenate([-sin_tab, sin_tab], axis=-1)
        cap = jnp.where(positions[:, None] >= jnp.arange(seq_len)[None, :], jnp.inf, -jnp.inf).astype(F32)
        hid = hidden.reshape(tokens, width)
        dout = d_out.reshape(tokens, width)
        k_proj = jnp.einsum('bld,de->ble', hidden, w_key, preferred_element_type=F32).astype(BF16)
        v_proj = jnp.einsum('bld,de->ble', hidden, w_value, preferred_element_type=F32).astype(BF16)
        k_rot = rotate(k_proj.astype(F32), cos_tab, sin_tab).astype(BF16)
        kv_all = lax.all_gather(jnp.stack([k_rot, v_proj]), 'sp')
        q = jnp.einsum('td,dhe->hte', hid, w_query, preferred_element_type=F32).astype(BF16)
        do = jnp.einsum('td,hed->hte', dout, w_out, preferred_element_type=F32).astype(BF16)
        o, dq, dkv = attention(q, do, kv_all, cos_full, sin_full, cap, score_scale)
        grad_w_out = lax.psum(jnp.einsum('hte,td->hed', o, dout, preferred_element_type=F32), 'sp')
        grad_w_query = lax.psum(jnp.einsum('td,hte->dhe', hid, dq, preferred_element_type=F32), 'sp')
        kv_grad = lax.psum_scatter(dkv, 'sp', scatter_dimension=0, tiled=False).astype(BF16)
        attn_out = jnp.einsum('hte,hed->td', o, w_out, preferred_element_type=F32).astype(BF16).reshape(hidden.shape)
        d_key = rotate_back(kv_grad[0].astype(F32), cos_tab, sin_tab).astype(BF16)
        d_value = kv_grad[1]
        d_hidden = (jnp.einsum('hte,dhe->td', dq, w_query, preferred_element_type=F32).reshape(hidden.shape) + jnp.einsum('ble,de->bld', d_key, w_key, preferred_element_type=F32) + jnp.einsum('ble,de->bld', d_value, w_value, preferred_element_type=F32)).astype(BF16)
        grad_w_key = jnp.einsum('bld,ble->de', hidden, d_key, preferred_element_type=F32)
        grad_w_value = jnp.einsum('bld,ble->de', hidden, d_value, preferred_element_type=F32)
        grad_w_key, grad_w_value = lax.psum((grad_w_key, grad_w_value), 'sp')
        return (attn_out, d_hidden, grad_w_query, grad_w_key, grad_w_value, grad_w_out)

    return jax.shard_map(local_step, mesh=mesh, in_specs=(seq_spec, seq_spec, rep_spec, rep_spec, rep_spec, rep_spec), out_specs=(seq_spec, seq_spec, rep_spec, rep_spec, rep_spec, rep_spec), check_vma=False)
```

time: 1020 us -> 704 us (0.69); the launches traced: 1010 us -> 704 us
  matrix products: 262 us -> 93.2 us
  waiting for transfers between devices: 584 us -> 477 us
  Pallas kernels: 0 us -> 82 us
  local copies, waits for them, and re-layouts: 83.2 us -> 34.3 us
  other arithmetic: 46.4 us -> 3.21 us
  starting transfers between devices: 17.6 us -> 0.52 us
    all_to_all x4 -> x0, waiting for transfers between devices: 273 us -> none  [the longest x1 87.9 us: local_step(): attn = lax.all_to_all(attn_heads, 'sp', 1, 2, tiled=True)]
    dot_general x18 -> x12, matrix products: 262 us -> 93.2 us  [the longest x1 15.5 us: local_step(): jnp.einsum('td,hte->dhe', hid, dq, preferred_element_type=F32)]
    reduce_scatter x1, waiting for transfers between devices: 11.7 us -> 150 us  [local_step(): lax.psum_scatter(dkv, 'sp', scatter_dimension=0, tiled=False).astype(BF16)]
    pallas_call x0 -> x1, Pallas kernels: none -> 82 us  [attention(): pl.pallas_call(functools.partial(attn_kernel, 4, scale), grid=(batch,), i...]
    all_gather x1, waiting for transfers between devices: 0.01 us -> 25.2 us  [local_step(): kv_all = lax.all_gather(jnp.stack([k_rot, v_proj]), 'sp')]
    convert_element_type x4 -> x0, local copies, waits for them, and re-layouts: 23.1 us -> none  [the longest x1 6.81 us: local_step(): jnp.einsum('bhqk,bke->bqhe', prob_half, v_full, preferred_element_type=jn...]
    reduce_sum x1 -> x0, other arithmetic: 21.6 us -> none  [causal_softmax(): return expo_vals / jnp.sum(expo_vals, axis=-1, keepdims=True)]
    another operation x5 -> x2, other arithmetic: 20.2 us -> 1.22 us  [the longest x1 0.97 us: local_step(): kv_all = lax.all_gather(jnp.stack([k_rot, v_proj]), 'sp')]
  transfers between devices with their start and end apart: 7 -> 3, of which waited for: 6 -> 3; matrix products, arithmetic and copies ran while one was open for 16% -> 12% of each run, Pallas kernels for 0% -> 0%
where the time goes in v1:
time: 704 us
  waiting for transfers between devices  477 us (68%)
  matrix products  93.2 us (13%)
  Pallas kernels  82 us (12%)
  local copies, waits for them, and re-layouts  34.3 us (5%)
  between operations  14 us (2%)
    psum x1, waiting for transfers between devices, local_step(): lax.psum(jnp.einsum('td,hte->dhe', hid, dq, preferred_element_type=F32),...  301 us
    reduce_scatter x1, waiting for transfers between devices, local_step(): lax.psum_scatter(dkv, 'sp', scatter_dimension=0, tiled=False).astype(BF16)  150 us
    pallas_call x1, Pallas kernels, attention(): pl.pallas_call(functools.partial(attn_kernel, 4, scale), grid=(batch,), i...  82 us
    unnamed x26, local copies, waits for them, and re-layouts  34.3 us
    all_gather x1, waiting for transfers between devices, local_step(): kv_all = lax.all_gather(jnp.stack([k_rot, v_proj]), 'sp')  25.2 us
    dot_general x1, matrix products, local_step(): jnp.einsum('td,hte->dhe', hid, dq, preferred_element_type=F32)  15.5 us
  transfers between devices with their start and end apart: 3, of which 3 were waited for; matrix products, arithmetic and copies ran while one was open for 12% of the time, Pallas kernels for 0%

profile of v1, /device:TPU:0, one launch (start us, length us, event | category | flops | bytes accessed | tf_op | source)
XLA Modules:
  0.0 703.7 jit_solution(7906292473464377105)
XLA Ops:
  7.2 0.0 all-gather.3.cloned.1.call-start
  7.3 3.7 fusion.7
  11.0 1.2 fusion.6
  12.3 0.2 fusion.17
  12.5 0.3 fusion.13
  12.7 1.0 pad_maximum_fusion
  13.7 0.0 all-gather.3.cloned.1.call-update
  13.7 0.2 reduce-scatter.2.cloned.1.call-start
  14.0 0.1 pad_maximum_fusion.4
  14.0 0.1 fusion.16.cap_ref
  14.1 13.4 %convert_bitcast_fusion.do_ref = bf16[16,1024,128]{2,1,0:T(8,128)(2,1)} fusion(bf16[16,128,2048]{2,1,0:T(8,128)(2,1)} %param.11, bf16[1024,2048,1]{1,0,2:T(8,128)(2,1)} %bitcast.70), kind=kOutput, calls=%fused_computation.7 | convolution fusion | flops 8592031744 | bytes 16777216 | tf_op jit(solution)/shard_map/td,hed->hte/dot_general | solution.py:124
  27.6 12.6 %convert_bitcast_fusion.1.q_ref = bf16[16,1024,128]{2,1,0:T(8,128)(2,1)} fusion(bf16[1024,2048,1]{1,0,2:T(8,128)(2,1)S(1)} %bitcast.67, bf16[2048,16,128]{2,1,0:T(8,128)(2,1)} %param.8), kind=kOutput, calls=%fused_computation.8 | convolution fusion | flops 8592031744 | bytes 16777216 | tf_op jit(solution)/shard_map/td,dhe->hte/dot_general | solution.py:123
  40.2 25.2 %all-gather.3.cloned.1.call-done = bf16[32,16,64,128]{3,2,1,0:T(8,128)(2,1)} async-done(((bf16[2,16,64,128]{3,2,1,0:T(8,128)(2,1)}), bf16[32,16,64,128]{3,2,1,0:T(8,128)(2,1)}) %all-gather.3.cloned.1.call-update) | async-done | bytes 8388624 | tf_op jit(solution)/shard_map/all_gather | solution.py:122
  65.3 82.0 %attn.1 = (bf16[16,1024,128]{2,1,0:T(8,128)(2,1)S(1)}, bf16[16,1024,128]{2,1,0:T(8,128)(2,1)}, f32[16,2,16,64,128]{4,3,2,1,0:T(8,128)}) custom-call(bf16[16,1024,128]{2,1,0:T(8,128)(2,1)} %convert_bitcast_fusion.1.q_ref, bf16[16,1024,128]{2,1,0:T(8,128)(2,1)} %convert_bitcast_fusion.do_ref, bf16[16,2,16,64,128]{4,3,2,1,0:T(8,128)(2,1)} %bitcast.69, ...), custom_call_target="tpu_custom_call" | custom-call | flops 25769803776 | bytes 41943040 | tf_op jit(solution)/shard_map/attn/pallas_call | solution.py:84
  147.3 2.0 copy-done.1
  149.3 0.3 all-reduce.3.cloned.1.call-start
  149.6 15.5 %convolution_bitcast_fusion = f32[2048,16,128]{0,2,1:T(8,128)} fusion(bf16[16,1024,128]{2,1,0:T(8,128)(2,1)} %get-tuple-element.10, bf16[1024,2048,1]{1,0,2:T(8,128)(2,1)} %bitcast.66), kind=kOutput, calls=%fused_computation.6 | convolution fusion | flops 8589934592 | bytes 25165824 | tf_op jit(solution)/shard_map/td,hte->dhe/dot_general | solution.py:127
  165.2 11.6 %fusion.21 = f32[16,128,2048]{2,1,0:T(8,128)} fusion(bf16[16,1024,128]{2,1,0:T(8,128)(2,1)S(1)} %copy-done.2, bf16[1024,2048,1]{1,0,2:T(8,128)(2,1)S(1)} %bitcast.71), kind=kOutput, calls=%fused_computation.43 | convolution fusion | flops 8589934592 | bytes 25165824 | tf_op jit(solution)/shard_map/hte,td->hed/dot_general | solution.py:126
  176.8 150.0 %reduce-scatter.2.cloned.1.call-done = f32[1,2,16,64,128]{4,3,2,1,0:T(8,128)} async-done(((f32[16,2,16,64,128]{4,3,2,1,0:T(8,128)}), f32[1,2,16,64,128]{4,3,2,1,0:T(8,128)}) %reduce-scatter.2.cloned.1.call-update) | async-done | bytes 1048592 | tf_op jit(solution)/shard_map/reduce_scatter | solution.py:128
  326.8 1.3 convert_element_type.69
  328.2 4.1 convolution_bitcast_fusion.1
  332.2 0.3 add_convert_fusion.1
  332.5 1.8 convolution_bitcast_fusion.2
  334.3 13.3 %bitcast_convert_fusion = bf16[1024,2048]{1,0:T(8,128)(2,1)} fusion(bf16[16,1024,128]{2,1,0:T(8,128)(2,1)} %copy-done.1, bf16[16,128,2048]{2,1,0:T(8,128)(2,1)} %param.11), kind=kOutput, calls=%fused_computation | convolution fusion | flops 8592031744 | bytes 16777216 | tf_op jit(solution)/shard_map/hte,hed->td/dot_general | solution.py:129
  347.7 11.4 %fusion.2 = f32[1024,2048,1]{1,0,2:T(8,128)S(1)} fusion(bf16[16,1024,128]{2,1,0:T(8,128)(2,1)S(1)} %copy-done.10, bf16[2048,16,128]{2,1,0:T(8,128)(2,1)} %param.8), kind=kOutput, calls=%fused_computation.4 | convolution fusion | flops 8589934592 | bytes 20971520 | tf_op jit(solution)/shard_map/hte,dhe->td/dot_general | solution.py:132
  359.0 1.3 fusion.10
  360.4 3.3 add_convert_fusion
  363.6 301.4 %all-reduce.3.cloned.1.call-done = (f32[2048,16,128]{0,2,1:T(8,128)}, f32[2048,128]{0,1:T(8,128)}, f32[2048,128]{0,1:T(8,128)}, f32[16,128,2048]{2,1,0:T(8,128)}) async-done(((f32[2048,16,128]{0,2,1:T(8,128)}, f32[2048,128]{0,1:T(8,128)}, f32[2048,128]{0,1:T(8,128)}, f32[16,128,2048]{2,1,0:T(8,128)}), (f32[2048,16,128]{0,2,1:T(8,128)}, f32[2048,128]{0,1:T(8,128)}, f32[2048,128]{0,1:T(8,128)}, ...) | async-done | bytes 35651600 | tf_op jit(solution)/shard_map/psum | solution.py:127
  665.0 17.8 %copy.27 = f32[2048,16,128]{2,1,0:T(8,128)} copy(f32[2048,16,128]{0,2,1:T(8,128)} %get-tuple-element.24) | data formatting | bytes 33554432
  682.8 1.3 copy.28
  684.1 1.3 copy.29
  685.4 11.8 %copy.44 = f32[16,128,2048]{2,1,0:T(8,128)} copy(f32[16,128,2048]{2,1,0:T(8,128)} %get-tuple-element.42) | data formatting | bytes 33554432
  (27 shorter events, 0.2 us)
Async XLA Ops:
  7.2 3.8 copy-start
  7.2 58.2 %all-gather.3.cloned.1.call-start = ((), (), s32[]{:S(2)}) async-start(), calls=%async_computation.2 | async-start | bytes 8912896 | tf_op jit(solution)/shard_map/all_gather | solution.py:122
  7.2 3.7 copy-start.3
  13.7 313.1 %reduce-scatter.2.cloned.1.call-start = ((), (), s32[]{:S(2)}) async-start(), calls=%async_computation.1 | async-start | bytes 17825792 | tf_op jit(solution)/shard_map/reduce_scatter | solution.py:128
  14.1 13.5 %copy-start.4 = (bf16[16,64,2048]{2,1,0:T(8,128)(2,1)S(1)}, bf16[16,64,2048]{2,1,0:T(8,128)(2,1)}, u32[]{:S(2)}) copy-start(bf16[16,64,2048]{2,1,0:T(8,128)(2,1)} %param.6) | copy-start | bytes 12582916
  147.3 2.0 copy-start.1
  149.3 515.7 %all-reduce.3.cloned.1.call-start = ((), (), s32[]{:S(2)}) async-start(), calls=%async_computation.3 | async-start | bytes 71303168 | tf_op jit(solution)/shard_map/psum | solution.py:127
  149.6 15.6 %copy-start.2 = (bf16[16,1024,128]{2,1,0:T(8,128)(2,1)S(1)}, bf16[16,1024,128]{2,1,0:T(8,128)(2,1)}, u32[]{:S(2)}) copy-start(bf16[16,1024,128]{2,1,0:T(8,128)(2,1)} %copy-done.1) | copy-start | bytes 12582916
  149.6 15.5 %copy-start.9 = (bf16[16,64,2048]{2,1,0:T(8,128)(2,1)S(1)}, bf16[16,64,2048]{2,1,0:T(8,128)(2,1)}, u32[]{:S(2)}) copy-start(bf16[16,64,2048]{2,1,0:T(8,128)(2,1)} %param.7) | copy-start | bytes 12582916
  328.1 4.4 copy-start.5
  334.3 13.3 %copy-start.10 = (bf16[16,1024,128]{2,1,0:T(8,128)(2,1)S(1)}, bf16[16,1024,128]{2,1,0:T(8,128)(2,1)}, u32[]{:S(2)}) copy-start(bf16[16,1024,128]{2,1,0:T(8,128)(2,1)} %get-tuple-element.10) | copy-start | bytes 12582916
  359.0 1.3 copy-start.8
  665.0 17.8 %copy-start.7 = (f32[2048,128]{0,1:T(8,128)S(1)}, f32[2048,128]{0,1:T(8,128)}, u32[]{:S(2)}) copy-start(f32[2048,128]{0,1:T(8,128)} %get-tuple-element.25) | copy-start | bytes 3145732
  665.0 19.1 %copy-start.6 = (f32[2048,128]{0,1:T(8,128)S(1)}, f32[2048,128]{0,1:T(8,128)}, u32[]{:S(2)}) copy-start(f32[2048,128]{0,1:T(8,128)} %get-tuple-element.26) | copy-start | bytes 3145732
Sparse Core Ops, SparseCore 0:
  13.8 51.4 all-gather.2
  149.5 177.2 reduce-scatter.1
  334.4 330.5 all-reduce.2

commit v2 on v1

--- a/solution.py
+++ b/solution.py
@@ -98,6 +98,221 @@
     )(q, do, kv_all, cos_tab, sin_tab, cap)
 
 
+MESH = pl.DeviceIdType.MESH
+COLORS = ((1, 2, 4), (2, 4, 1), (4, 1, 2))
+ORDER = (7, 3, 6, 5, 1, 2, 4, 0)
+
+
+class Place:
+    def __init__(self):
+        me = lax.axis_index('sp')
+        self.core = me % 2
+        self.bits = ((me // 2) % 2, (me // 4) % 2, me // 8)
+
+    def chip(self, rel):
+        x, y, z = [1 - b if rel >> i & 1 else b for i, b in enumerate(self.bits)]
+        return z * 4 + y * 2 + x
+
+    def device(self, rel, other_core=False):
+        return self.chip(rel) * 2 + (1 - self.core if other_core else self.core)
+
+
+class Copies:
+    def __init__(self, send_sem, recv_sem):
+        self.send_sem, self.recv_sem = send_sem, recv_sem
+        self.started, self.n = [], 0
+
+    def remote(self, src, dst, device):
+        copy = pltpu.make_async_remote_copy(src_ref=src, dst_ref=dst, send_sem=self.send_sem.at[self.n], recv_sem=self.recv_sem.at[self.n],
+                                            device_id=(device,), device_id_type=MESH)
+        self.n += 1
+        copy.start()
+        self.started.append(copy.wait_send)
+        return copy
+
+    def local(self, src, dst):
+        copy = pltpu.make_async_copy(src, dst, self.send_sem.at[self.n])
+        self.n += 1
+        copy.start()
+        return copy
+
+    def finish(self):
+        for wait in self.started:
+            wait()
+
+
+def entry_barrier(place):
+    barrier = pltpu.get_barrier_semaphore()
+    for device in (place.device(0, True), place.device(1), place.device(2), place.device(4)):
+        pl.semaphore_signal(barrier, inc=1, device_id=(device,), device_id_type=MESH)
+    pl.semaphore_wait(barrier, 4)
+
+
+def add_into(dst, src):
+    dst[...] += src[...]
+
+
+class Halving:
+    def __init__(self, place, copies, own, r1, r2, r3):
+        self.place, self.copies, self.own = place, copies, own
+        self.recv = (r1, r2, r3)
+        self.arrive = {}
+
+    def slots(self, color, stage):
+        m1, m2, m3 = COLORS[color]
+        return ((m2, m2 | m3, m3, 0), (m3, 0), (0,))[stage]
+
+    def send(self, rel, color, stage):
+        mask = COLORS[color][stage]
+        landed = rel ^ mask
+        slot = self.slots(color, stage).index(landed)
+        dst = self.recv[stage].at[slot, self.part(color)]
+        self.arrive[(stage, color, landed)] = (self.copies.remote(self.own(rel, color), dst, self.place.device(mask)), dst)
+
+    def part(self, color):
+        return self.parts[color]
+
+    def ready(self, rel):
+        for color in range(3):
+            if rel & COLORS[color][0]:
+                self.send(rel, color, 0)
+
+    def run(self):
+        for stage in range(3):
+            for i in range((4, 2, 1)[stage]):
+                for color in range(3):
+                    rel = self.slots(color, stage)[i]
+                    copy, landed = self.arrive[(stage, color, rel)]
+                    copy.wait_recv()
+                    add_into(self.own(rel, color), landed)
+                    if stage < 2 and rel & COLORS[color][stage + 1]:
+                        self.send(rel, color, stage + 1)
+
+
+def kv_reduce_kernel(parts, x_ref, out_ref, acc, recv0, r1, r2, r3, send_sem, recv_sem):
+    place = Place()
+    copies = Copies(send_sem, recv_sem)
+    entry_barrier(place)
+    loads, d2d = {}, {}
+    for rel in ORDER:
+        d2d[rel] = copies.remote(x_ref.at[place.device(rel, True)], recv0.at[rel], place.device(0, True))
+        loads[rel] = copies.local(x_ref.at[place.device(rel)], acc.at[rel])
+    halving = Halving(place, copies, lambda rel, color: acc.at[rel, parts[color]], r1, r2, r3)
+    halving.parts = parts
+    for rel in ORDER:
+        loads[rel].wait()
+        d2d[rel].wait_recv()
+        add_into(acc.at[rel], recv0.at[rel])
+        halving.ready(rel)
+    halving.run()
+    out_ref[...] = acc[0].astype(BF16)
+    copies.finish()
+
+
+def kv_reduce(x):
+    ndev, slabs, rows, dim = x.shape
+    third = -(-slabs // 3)
+    parts = tuple(pl.ds(c * third, min(third, slabs - c * third)) for c in range(3))
+    buf = lambda n: pltpu.VMEM((n, slabs, rows, dim), F32)
+    return pl.pallas_call(
+        functools.partial(kv_reduce_kernel, parts),
+        out_shape=jax.ShapeDtypeStruct((slabs, rows, dim), BF16),
+        in_specs=[pl.BlockSpec(memory_space=pl.ANY)],
+        out_specs=pl.BlockSpec(memory_space=pltpu.VMEM),
+        scratch_shapes=[buf(8), buf(8), buf(4), buf(2), buf(1), pltpu.SemaphoreType.DMA((40,)), pltpu.SemaphoreType.DMA((40,))],
+        compiler_params=pltpu.CompilerParams(collective_id=0, has_side_effects=True, vmem_limit_bytes=48 * 1024 * 1024),
+        cost_estimate=pl.CostEstimate(flops=1_000_000, bytes_accessed=32 * 1024 * 1024, transcendentals=0),
+        name="kv_reduce",
+    )(x)
+
+
+def weight_grads_kernel(hid_ref, dq_ref, dkv_ref, out_ref, x, recv0, r1, r2, r3, gat, send_sem, recv_sem):
+    place = Place()
+    core = place.core
+    copies = Copies(send_sem, recv_sem)
+    entry_barrier(place)
+    heads, tokens, dim = dq_ref.shape
+    slabs = x.shape[2]
+    wide, small = dim, dim // heads
+    parts = tuple(pl.ds(c * (slabs // 3), slabs // 3) for c in range(3))
+    halving = Halving(place, copies, lambda rel, color: x.at[rel, core, parts[color]], r1, r2, r3)
+    halving.parts = parts
+
+    def partial_block(rel):
+        cols = pl.ds(pl.multiple_of(place.chip(rel) * 2 * dim, 2 * dim), 2 * dim)
+        hid_t = hid_ref[:, cols].T
+        for pair in range(heads // 2):
+            rhs = jnp.concatenate([dq_ref[2 * pair], dq_ref[2 * pair + 1]], axis=1)
+            g = jnp.dot(hid_t, rhs, preferred_element_type=F32)
+            for i in range(2):
+                for h in range(2):
+                    x[rel, i, 0:wide, 2 * pair + h, :] = g[i * dim:(i + 1) * dim, h * dim:(h + 1) * dim]
+        g = jnp.dot(hid_t, dkv_ref[...], preferred_element_type=F32)
+        for i in range(2):
+            for h in range(2):
+                x[rel, i, wide + h * small:wide + (h + 1) * small] = g[i * dim:(i + 1) * dim, h * dim:(h + 1) * dim].reshape(small, heads, dim)
+
+    d2d = {}
+
+    def paired(rel):
+        d2d[rel].wait_recv()
+        add_into(x.at[rel, core], recv0.at[rel])
+        halving.ready(rel)
+
+    last = None
+    for rel in ORDER:
+        partial_block(rel)
+        d2d[rel] = copies.remote(x.at[rel, 1 - core], recv0.at[rel], place.device(0, True))
+        if last is not None:
+            paired(last)
+        last = rel
+    paired(last)
+    halving.run()
+
+    arrive, tail = {}, []
+
+    def have(rel, color, src):
+        m1, m2, m3 = COLORS[color]
+        masks = (m3, m2, m1) if rel == 0 else (m2, m1) if rel == m3 else (m1,) if rel in (m2, m2 | m3) else ()
+        for mask in masks:
+            landed = rel | mask
+            dst = gat.at[landed, parts[color]]
+            arrive[(color, landed)] = (copies.remote(src, dst, place.device(mask)), dst)
+        home = out_ref.at[place.device(rel), parts[color]]
+        tail.append(copies.local(src, home).wait)
+        tail.append(copies.remote(src, home, place.device(0, True)).wait_recv)
+
+    for color in range(3):
+        have(0, color, x.at[0, core, parts[color]])
+    for step in range(7):
+        for color in range(3):
+            m1, m2, m3 = COLORS[color]
+            rel = (m3, m2, m1, m2 | m3, m1 | m3, m1 | m2, 7)[step]
+            copy, landed = arrive[(color, rel)]
+            copy.wait_recv()
+            have(rel, color, landed)
+    for wait in tail:
+        wait()
+    copies.finish()
+
+
+def weight_grads(hid, dq, dkv):
+    heads, tokens, dim = dq.shape
+    slabs = dim + 2 * (dim // heads)
+    buf = lambda *n: pltpu.VMEM((*n, slabs, heads, dim), F32)
+    vmem = pl.BlockSpec(memory_space=pltpu.VMEM)
+    return pl.pallas_call(
+        weight_grads_kernel,
+        out_shape=jax.ShapeDtypeStruct((16, slabs, heads, dim), F32),
+        in_specs=[vmem, vmem, vmem],
+        out_specs=pl.BlockSpec(memory_space=pl.ANY),
+        scratch_shapes=[buf(8, 2), buf(8), buf(4), buf(2), buf(1), buf(8), pltpu.SemaphoreType.DMA((128,)), pltpu.SemaphoreType.DMA((128,))],
+        compiler_params=pltpu.CompilerParams(collective_id=1, has_side_effects=True, vmem_limit_bytes=63 * 1024 * 1024),
+        cost_estimate=pl.CostEstimate(flops=1_000_000, bytes_accessed=64 * 1024 * 1024, transcendentals=0),
+        name="weight_grads",
+    )(hid, dq, dkv)
+
+
 def solution(mesh):
     axis_size = mesh.shape['sp']
     seq_spec = P(None, 'sp', None)
@@ -106,6 +321,7 @@
     def local_step(hidden, d_out, w_query, w_key, w_value, w_out):
         batch, local_len, width = hidden.shape
         head_dim = w_key.shape[1]
+        num_heads = w_query.shape[1]
         seq_len = local_len * axis_size
         tokens = batch * local_len
         score_scale = head_dim ** -0.5
@@ -123,16 +339,19 @@
         q = jnp.einsum('td,dhe->hte', hid, w_query, preferred_element_type=F32).astype(BF16)
         do = jnp.einsum('td,hed->hte', dout, w_out, preferred_element_type=F32).astype(BF16)
         o, dq, dkv = attention(q, do, kv_all, cos_full, sin_full, cap, score_scale)
-        grad_w_out = lax.psum(jnp.einsum('hte,td->hed', o, dout, preferred_element_type=F32), 'sp')
-        grad_w_query = lax.psum(jnp.einsum('td,hte->dhe', hid, dq, preferred_element_type=F32), 'sp')
-        kv_grad = lax.psum_scatter(dkv, 'sp', scatter_dimension=0, tiled=False).astype(BF16)
-        attn_out = jnp.einsum('hte,hed->td', o, w_out, preferred_element_type=F32).astype(BF16).reshape(hidden.shape)
+        grad_out_part, dkv = lax.optimization_barrier((jnp.einsum('hte,td->hed', o, dout, preferred_element_type=F32), dkv))
+        grad_w_out = lax.psum(grad_out_part, 'sp')
+        kv_grad = kv_reduce(dkv.reshape(axis_size, 2 * batch, local_len, head_dim)).reshape(2, batch, local_len, head_dim)
         d_key = rotate_back(kv_grad[0].astype(F32), cos_tab, sin_tab).astype(BF16)
         d_value = kv_grad[1]
+        dkv_tok = jnp.concatenate([d_key, d_value], axis=-1).reshape(tokens, 2 * head_dim)
+        grads = weight_grads(hid, dq, dkv_tok)
+        per = head_dim // num_heads
+        grad_w_query = grads[:, :head_dim].reshape(width, num_heads, head_dim)
+        grad_w_key = grads[:, head_dim:head_dim + per].reshape(width, head_dim)
+        grad_w_value = grads[:, head_dim + per:].reshape(width, head_dim)
+        attn_out = jnp.einsum('hte,hed->td', o, w_out, preferred_element_type=F32).astype(BF16).reshape(hidden.shape)
         d_hidden = (jnp.einsum('hte,dhe->td', dq, w_query, preferred_element_type=F32).reshape(hidden.shape) + jnp.einsum('ble,de->bld', d_key, w_key, preferred_element_type=F32) + jnp.einsum('ble,de->bld', d_value, w_value, preferred_element_type=F32)).astype(BF16)
-        grad_w_key = jnp.einsum('bld,ble->de', hidden, d_key, preferred_element_type=F32)
-        grad_w_value = jnp.einsum('bld,ble->de', hidden, d_value, preferred_element_type=F32)
-        grad_w_key, grad_w_value = lax.psum((grad_w_key, grad_w_value), 'sp')
         return (attn_out, d_hidden, grad_w_query, grad_w_key, grad_w_value, grad_w_out)
 
     return jax.shard_map(local_step, mesh=mesh, in_specs=(seq_spec, seq_spec, rep_spec, rep_spec, rep_spec, rep_spec), out_specs=(seq_spec, seq_spec, rep_spec, rep_spec, rep_spec, rep_spec), check_vma=False)

time: 704 us -> 555 us (0.79)
  waiting for transfers between devices: 477 us -> 25.2 us
  Pallas kernels: 82 us -> 406 us
  matrix products: 93.2 us -> 72.8 us
    pallas_call x0 -> x2, Pallas kernels: none -> 324 us  [the longest x1 212 us: weight_grads(): pl.pallas_call(weight_grads_kernel, out_shape=jax.ShapeDtypeStruct((16, s...]
    psum x1, waiting for transfers between devices: 301 us -> 0.01 us  [local_step(): grad_w_out = lax.psum(grad_out_part, 'sp')]
    reduce_scatter x1 -> x0, waiting for transfers between devices: 150 us -> none  [local_step(): lax.psum_scatter(dkv, 'sp', scatter_dimension=0, tiled=False).astype(BF16)]
    dot_general x3 -> x0, matrix products: 21.4 us -> none  [the longest x1 15.5 us: local_step(): jnp.einsum('td,hte->dhe', hid, dq, preferred_element_type=F32)]
    unnamed x26 -> x23, local copies, waits for them, and re-layouts: 34.3 us -> 15.3 us
    slice x0 -> x2, local copies, waits for them, and re-layouts: none -> 14.9 us  [the longest x1 11.7 us: local_step(): grad_w_query = grads[:, :head_dim].reshape(width, num_heads, head_dim)]
  transfers between devices with their start and end apart: 3 -> 2, of which waited for: 3 -> 1; matrix products, arithmetic and copies ran while one was open for 12% -> 13% of each run, Pallas kernels for 0% -> 59%
where the time goes in v2:
time: 555 us; the launch traced here: 552 us
  Pallas kernels  406 us (73%)
  matrix products  72.8 us (13%)
  local copies, waits for them, and re-layouts  30.2 us (5%)
  waiting for transfers between devices  25.2 us (5%)
  between operations  14.4 us (3%)
    pallas_call x1, Pallas kernels, weight_grads(): pl.pallas_call(weight_grads_kernel, out_shape=jax.ShapeDtypeStruct((16, s...  212 us
    pallas_call x1, Pallas kernels, kv_reduce(): pl.pallas_call(functools.partial(kv_reduce_kernel, parts), out_shape=jax....  113 us
    pallas_call x1, Pallas kernels, attention(): pl.pallas_call(functools.partial(attn_kernel, 4, scale), grid=(batch,), i...  82.1 us
    all_gather x1, waiting for transfers between devices, local_step(): kv_all = lax.all_gather(jnp.stack([k_rot, v_proj]), 'sp')  25.2 us
    unnamed x23, local copies, waits for them, and re-layouts  15.3 us
    dot_general x1, matrix products, local_step(): jnp.einsum('td,hed->hte', dout, w_out, preferred_element_type=F32)  13.4 us
    dot_general x1, matrix products, local_step(): jnp.einsum('td,dhe->hte', hid, w_query, preferred_element_type=F32)  12.6 us
    dot_general x1, matrix products, local_step(): jnp.einsum('hte,hed->td', o, w_out, preferred_element_type=F32).astype(BF16)  11.9 us
  transfers between devices with their start and end apart: 2, of which 1 were waited for; matrix products, arithmetic and copies ran while one was open for 13% of the time, Pallas kernels for 59%

profile of v2, /device:TPU:0, one launch (start us, length us, event | category | flops | bytes accessed | tf_op | source)
XLA Modules:
  0.0 552.3 jit_solution(13783732107844360559)
XLA Ops:
  7.2 0.0 copy-start
  7.2 0.0 all-gather.3.cloned.1.call-start
  7.3 3.6 fusion.7
  10.9 3.4 fusion.6
  14.3 0.2 fusion.19
  14.5 0.3 fusion.13
  14.8 1.0 pad_maximum_fusion
  15.7 0.0 all-gather.3.cloned.1.call-update
  15.8 0.2 all-reduce.2.cloned.1.call-start
  16.0 0.1 pad_maximum_fusion.2
  16.1 0.1 fusion.18.cap_ref
  16.2 13.4 %convert_bitcast_fusion.do_ref = bf16[16,1024,128]{2,1,0:T(8,128)(2,1)} fusion(bf16[16,128,2048]{2,1,0:T(8,128)(2,1)} %param.11, bf16[1024,2048,1]{1,0,2:T(8,128)(2,1)} %bitcast.58), kind=kOutput, calls=%fused_computation.6 | convolution fusion | flops 8592031744 | bytes 16777216 | tf_op jit(solution)/shard_map/td,hed->hte/dot_general | solution.py:340
  29.6 12.6 %convert_bitcast_fusion.1.q_ref = bf16[16,1024,128]{2,1,0:T(8,128)(2,1)} fusion(bf16[1024,2048,1]{1,0,2:T(8,128)(2,1)S(1)} %bitcast.52, bf16[2048,16,128]{2,1,0:T(8,128)(2,1)} %param.8), kind=kOutput, calls=%fused_computation.7 | convolution fusion | flops 8592031744 | bytes 16777216 | tf_op jit(solution)/shard_map/td,dhe->hte/dot_general | solution.py:339
  42.2 25.2 %all-gather.3.cloned.1.call-done = bf16[32,16,64,128]{3,2,1,0:T(8,128)(2,1)} async-done(((bf16[2,16,64,128]{3,2,1,0:T(8,128)(2,1)}), bf16[32,16,64,128]{3,2,1,0:T(8,128)(2,1)}) %all-gather.3.cloned.1.call-update) | async-done | bytes 8388624 | tf_op jit(solution)/shard_map/all_gather | solution.py:338
  67.4 82.1 %attn.1 = (bf16[16,1024,128]{2,1,0:T(8,128)(2,1)S(1)}, bf16[16,1024,128]{2,1,0:T(8,128)(2,1)}, f32[16,2,16,64,128]{4,3,2,1,0:T(8,128)}) custom-call(bf16[16,1024,128]{2,1,0:T(8,128)(2,1)} %convert_bitcast_fusion.1.q_ref, bf16[16,1024,128]{2,1,0:T(8,128)(2,1)} %convert_bitcast_fusion.do_ref, bf16[16,2,16,64,128]{4,3,2,1,0:T(8,128)(2,1)} %bitcast.57, ...), custom_call_target="tpu_custom_call" | custom-call | flops 25769803776 | bytes 41943040 | tf_op jit(solution)/shard_map/attn/pallas_call | solution.py:84
  149.5 2.0 copy-done.3
  151.5 11.7 %fusion.24 = f32[16,128,2048]{2,1,0:T(8,128)} fusion(bf16[16,1024,128]{2,1,0:T(8,128)(2,1)S(1)} %get-tuple-element.11, bf16[1024,2048,1]{1,0,2:T(8,128)(2,1)S(1)} %bitcast.59), kind=kOutput, calls=%fused_computation.42 | convolution fusion | flops 8589934592 | bytes 25165824 | tf_op jit(solution)/shard_map/hte,td->hed/dot_general | solution.py:342
  163.2 0.0 all-reduce.2.cloned.1.call-update
  163.2 112.6 %kv_reduce.1 = bf16[32,64,128]{2,1,0:T(8,128)(2,1)S(1)} custom-call(f32[16,32,64,128]{3,2,1,0:T(8,128)} %bitcast.50), custom_call_target="tpu_custom_call" | custom-call | flops 1000000 | bytes 33554432 | tf_op jit(solution)/shard_map/kv_reduce/pallas_call | solution.py:217
  275.8 0.8 copy-done.1
  276.6 0.1 fusion.23
  276.6 0.3 add_convert_fusion.1
  276.9 0.7 copy-done.7
  277.6 1.0 pad_maximum_fusion.1
  278.6 211.7 %weight_grads.1 = f32[16,144,16,128]{3,2,1,0:T(8,128)} custom-call(bf16[1024,2048]{1,0:T(8,128)(2,1)} %bitcast.51, bf16[16,1024,128]{2,1,0:T(8,128)(2,1)} %get-tuple-element.12.dq_ref, bf16[1024,256]{1,0:T(8,128)(2,1)} %bitcast.54), custom_call_target="tpu_custom_call" | custom-call | flops 1000000 | bytes 67108864 | tf_op jit(solution)/shard_map/weight_grads/pallas_call | solution.py:304
  490.4 11.7 %slice.35 = f32[16,128,16,128]{3,2,1,0:T(8,128)} slice(f32[16,144,16,128]{3,2,1,0:T(8,128)} %weight_grads.1), slice={[0:16], [0:128], [0:16], [0:128]} | slice | bytes 33554432 | tf_op jit(solution)/shard_map/slice | solution.py:350
  502.0 3.2 fusion.22
  505.3 1.3 fusion.10
  506.6 11.6 %fusion.2 = f32[1024,2048,1]{1,0,2:T(8,128)S(1)} fusion(bf16[16,1024,128]{2,1,0:T(8,128)(2,1)S(1)} %copy-done.6, bf16[2048,16,128]{2,1,0:T(8,128)(2,1)} %param.8), kind=kOutput, calls=%fused_computation.4 | convolution fusion | flops 8589934592 | bytes 20971520 | tf_op jit(solution)/shard_map/hte,dhe->td/dot_general | solution.py:354
  518.3 3.3 add_convert_fusion
  521.6 11.9 %bitcast_convert_fusion = bf16[1024,2048]{1,0:T(8,128)(2,1)} fusion(bf16[16,1024,128]{2,1,0:T(8,128)(2,1)S(1)} %copy-done.4, bf16[16,128,2048]{2,1,0:T(8,128)(2,1)} %param.11), kind=kOutput, calls=%fused_computation | convolution fusion | flops 8592031744 | bytes 16777216 | tf_op jit(solution)/shard_map/hte,hed->td/dot_general | solution.py:353
  533.4 11.8 %copy.32 = f32[16,128,2048]{2,1,0:T(8,128)} copy(f32[16,128,2048]{2,1,0:T(8,128)} %all-reduce.2.cloned.1.call-done) | data formatting | bytes 33554432
  (22 shorter events, 0.1 us)
Async XLA Ops:
  7.2 3.7 copy-start
  7.2 60.2 %all-gather.3.cloned.1.call-start = ((), (), s32[]{:S(2)}) async-start(), calls=%async_computation.1 | async-start | bytes 8912896 | tf_op jit(solution)/shard_map/all_gather | solution.py:338
  15.8 517.7 %all-reduce.2.cloned.1.call-start = ((), (), s32[]{:S(2)}) async-start(), calls=%async_computation | async-start | bytes 33554432 | tf_op jit(solution)/shard_map/psum | solution.py:343
  16.2 13.5 %copy-start.5 = (bf16[16,64,2048]{2,1,0:T(8,128)(2,1)S(1)}, bf16[16,64,2048]{2,1,0:T(8,128)(2,1)}, u32[]{:S(2)}) copy-start(bf16[16,64,2048]{2,1,0:T(8,128)(2,1)} %param.6) | copy-start | bytes 12582916
  67.4 84.1 %copy-start.10 = (bf16[16,64,2048]{2,1,0:T(8,128)(2,1)S(1)}, bf16[16,64,2048]{2,1,0:T(8,128)(2,1)}, u32[]{:S(2)}) copy-start(bf16[16,64,2048]{2,1,0:T(8,128)(2,1)} %param.7) | copy-start | bytes 12582916
  149.5 2.0 copy-start.3
  275.8 0.8 copy-start.1
  276.9 0.7 copy-start.7
  490.4 14.9 %copy-start.8 = (bf16[16,64,64]{2,1,0:T(8,128)(2,1)S(1)}, bf16[16,64,64]{2,1,0:T(8,128)(2,1)}, u32[]{:S(2)}) copy-start(bf16[16,64,64]{2,1,0:T(8,128)(2,1)} %copy-done.7) | copy-start | bytes 393220
  502.0 4.5 copy-start.6
  506.6 11.7 %copy-start.2 = (bf16[32,64,128]{2,1,0:T(8,128)(2,1)S(1)}, bf16[32,64,128]{2,1,0:T(8,128)(2,1)}, u32[]{:S(2)}) copy-start(bf16[32,64,128]{2,1,0:T(8,128)(2,1)} %copy-done.1) | copy-start | bytes 1572868
  506.6 11.7 %copy-start.9 = (bf16[2048,128]{1,0:T(8,128)(2,1)S(1)}, bf16[2048,128]{1,0:T(8,128)(2,1)}, u32[]{:S(2)}) copy-start(bf16[2048,128]{1,0:T(8,128)(2,1)} %param.10) | copy-start | bytes 1572868
  518.3 3.3 copy-start.4
Sparse Core Ops, SparseCore 0:
  15.9 51.4 all-gather.2
  163.3 302.3 all-reduce.1
